TPU v7x, 32 devices: a whole 2x2x4 slice. The times are simulated.
32 devices in a mesh: zero: 8 (over z, x), width: 4 (over y, core).
Axes of the slice: x: 2, y: 2, z: 4, core: 2. Of those that a mesh axis runs over, the one named last changes fastest.
Arguments:
- weight_up: bfloat16 [12288, 49152], P('zero', 'width'), may hold values from -0.078125 to 0.078125
- low_up: bfloat16 [12288, 64], P('zero'), may hold values from -0.0546875 to 0.0546875
- high_up: bfloat16 [64, 49152], P(None, 'width'), may hold values from -0.75 to 0.75
- norm_train: float32 [12288], P(('zero', 'width')), may hold values from 0.25 to 1.75
- norm_step: float32 [12288], P(('zero', 'width')), may hold values from -0.3 to 0.3
Outputs:
- ready_up: bfloat16 [12288, 49152], P(None, ('width', 'zero'))
- scale_up: float32 [49152], P(('width', 'zero'))
- serve_norm: bfloat16 [12288], replicated
All inputs are finite; a program needn't handle non-finite values. Where the computation divides by a largest or mean magnitude, that divisor is 1e-20 or more.
Results may differ from a plain program's by a relative error of at most 0.001.
Values may be sent and summed in bfloat16 or wider, within the bound.
A program may use at most 192 MiB of HBM per device.

v0:
```python
import jax
import jax.numpy as jnp
from jax import lax
from jax.sharding import PartitionSpec as P

mix_rate = 2.0


def shards(weight_up, low_up, high_up, norm_train, norm_step):
    latest_up = weight_up.astype(jnp.float32) + mix_rate * jnp.dot(
        low_up, high_up, preferred_element_type=jnp.float32
    )
    scale_up = lax.pmax(jnp.max(jnp.abs(latest_up), axis=0), "zero")
    narrow_up = (latest_up / scale_up).astype(jnp.bfloat16)
    ready_up = lax.all_to_all(narrow_up, "zero", split_axis=1, concat_axis=0, tiled=True)
    place = lax.axis_index("zero")
    scale_up = lax.dynamic_slice_in_dim(scale_up, place * ready_up.shape[1], ready_up.shape[1])
    serve_norm = lax.all_gather(
        (norm_train + norm_step).astype(jnp.bfloat16), ("zero", "width"), axis=0, tiled=True
    )
    return (ready_up, scale_up, serve_norm)


def solution(mesh):
    return jax.shard_map(
        shards,
        mesh=mesh,
        in_specs=(
            P("zero", "width"),
            P("zero", None),
            P(None, "width"),
            P(("zero", "width")),
            P(("zero", "width")),
        ),
        out_specs=(P(None, ("width", "zero")), P(("width", "zero")), P()),
        check_vma=False,
    )
```

profile of v0, /device:TPU:17, one launch (start us, length us, event | category | flops | bytes accessed | tf_op | source)
XLA Modules:
  0.0 1004.0 jit_solution(10228856172117339394)
XLA Ops:
  0.6 0.0 copy-start
  0.6 1.4 copy-done
  2.0 37.4 %abs_reduce_fusion = (f32[12288]{0:T(1024)S(1)}, f32[1536,12288]{1,0:T(8,128)}) fusion(bf16[1536,64]{0,1:T(8,128)(2,1)} %param.6, bf16[64,12288]{1,0:T(8,128)(2,1)S(1)} %copy-done, bf16[1536,12288]{1,0:T(8,128)(2,1)} %param.5), kind=kOutput, calls=%fused_computation.1 | convolution fusion | flops 2510278656 | bytes 115064832 | tf_op jit(solution)/shard_map/dot_general | solution.py:10
  39.4 25.9 %pmax.7 = f32[12288]{0:T(1024)S(1)} all-reduce(f32[12288]{0:T(1024)S(1)} %get-tuple-element.3), channel_id=1, replica_groups=mesh['zero'=8,'width'=4] {'zero'}, use_global_device_ids=true, to_apply=%region_1.0 | all-reduce | flops 12288 | bytes 98304 | tf_op jit(solution)/shard_map/pmax | solution.py:13
  65.3 36.5 %divide_convert_fusion = bf16[1536,12288]{1,0:T(8,128)(2,1)} fusion(f32[1536,12288]{1,0:T(8,128)} %get-tuple-element.4, f32[12288]{0:T(1024)S(1)} %pmax.7), kind=kLoop, calls=%fused_computation | loop fusion | flops 37748736 | bytes 113295360 | tf_op jit(solution)/shard_map/convert_element_type | solution.py:14
  101.8 26.0 %copy.13 = bf16[192,8,8,1536]{3,2,0,1:T(8,128)(2,1)} copy(bf16[192,8,8,1536]{3,2,1,0:T(8,128)(2,1)} %bitcast.10) | data formatting | bytes 75497472 | tf_op jit(solution)/shard_map/all_to_all | solution.py:15
  127.8 0.0 copy-start.2
  127.8 0.0 copy-start.3
  127.8 12.3 %all-to-all-start = ((bf16[1536,8,1536]{2,0,1:T(8,128)(2,1)}), bf16[1536,8,1536]{2,0,1:T(8,128)(2,1)}, u32[]{:S(2)}, u32[]{:S(2)}) async-start(bf16[1536,8,1536]{2,0,1:T(8,128)(2,1)} %bitcast.9), calls=%async_computation | async-start | bytes 75497472 | tf_op jit(solution)/shard_map/all_to_all | solution.py:15
  140.1 0.7 dynamic_slice.3
  140.7 0.0 copy-done.2
  140.8 0.0 copy-done.3
  140.8 836.7 %all-gather = bf16[32,1,384]{2,1,0:T(2,128)(2,1)S(1)} all-gather(bf16[1,1,384]{2,1,0:T(2,128)(2,1)S(1)} %reshape.10), channel_id=1, replica_groups=mesh['zero'=8,'width'=4] {'zero','width'}, dimensions={0}, use_global_device_ids=true | all-gather | bytes 25344 | tf_op jit(solution)/shard_map/all_gather | solution.py:18
  977.5 0.1 reduce
  977.6 0.6 reshape.11
  978.3 0.0 all-to-all-done
  978.3 0.0 copy-start.1
  978.3 25.7 %copy.15 = bf16[12288,1536]{1,0:T(8,128)(2,1)} copy(bf16[12288,1536]{1,0:T(8,128)(2,1)} %bitcast.1) | data formatting | bytes 75497472
  1004.0 0.0 copy-done.1
  (2 shorter events, 0.0 us)
Async XLA Ops:
  0.6 1.4 copy-start
  127.8 13.0 %copy-start.2 = (f32[384]{0:T(512)S(1)}, f32[384]{0:T(512)}, u32[]{:S(2)}) copy-start(f32[384]{0:T(512)} %param.8) | copy-start | bytes 4612
  127.8 13.0 %copy-start.3 = (f32[384]{0:T(512)S(1)}, f32[384]{0:T(512)}, u32[]{:S(2)}) copy-start(f32[384]{0:T(512)} %param.9) | copy-start | bytes 4612
  127.8 850.5 %all-to-all-start = ((bf16[1536,8,1536]{2,0,1:T(8,128)(2,1)}), bf16[1536,8,1536]{2,0,1:T(8,128)(2,1)}, u32[]{:S(2)}, u32[]{:S(2)}) async-start(bf16[1536,8,1536]{2,0,1:T(8,128)(2,1)} %bitcast.9), calls=%async_computation | async-start | bytes 75497472 | tf_op jit(solution)/shard_map/all_to_all | solution.py:15
  978.3 25.8 %copy-start.1 = (bf16[64,12288]{1,0:T(8,128)(2,1)S(1)}, bf16[64,12288]{1,0:T(8,128)(2,1)}, u32[]{:S(2)}) copy-start(bf16[64,12288]{1,0:T(8,128)(2,1)} %param.7) | copy-start | bytes 4718596
where the time goes:
time: 1000 us
  blocking collectives  863 us (86%)
  local copies, waits for them, and re-layouts  54.4 us (5%)
  matrix products  37.4 us (4%)
  other arithmetic  36.6 us (4%)
  starting transfers between devices  12.3 us (1%)
    all_gather x1, blocking collectives, shards(): lax.all_gather((norm_train + norm_step).astype(jnp.bfloat16), ('zero', 'w...  837 us
    dot_general x1, matrix products, shards(): jnp.dot(low_up, high_up, preferred_element_type=jnp.float32)  37.4 us
    convert_element_type x1, other arithmetic, shards(): narrow_up = (latest_up / scale_up).astype(jnp.bfloat16)  36.5 us
    unnamed x11, local copies, waits for them, and re-layouts  27.8 us
    all_to_all x1, local copies, waits for them, and re-layouts, shards(): lax.all_to_all(narrow_up, 'zero', split_axis=1, concat_axis=0, tiled=True)  26 us
    pmax x1, blocking collectives, shards(): scale_up = lax.pmax(jnp.max(jnp.abs(latest_up), axis=0), 'zero')  25.9 us
  transfers between devices with their start and end apart: 1, of which 0 were waited for; matrix products, arithmetic and copies ran while one was open for 0% of the time, Pallas kernels for 0%

commit v1 on v0

--- a/solution.py
+++ b/solution.py
@@ -1,12 +1,133 @@
+import functools
+
 import jax
 import jax.numpy as jnp
 from jax import lax
+from jax.experimental import pallas as pl
+from jax.experimental.pallas import tpu as pltpu
 from jax.sharding import PartitionSpec as P
+
 
 mix_rate = 2.0
 
 
-def shards(weight_up, low_up, high_up, norm_train, norm_step):
+def latest(weight_ref, low_ref, high_ref):
+    return weight_ref[...].astype(jnp.float32) + jnp.dot(
+        low_ref[...], high_ref[...], preferred_element_type=jnp.float32
+    )
+
+
+def top_kernel(place_ref, weight_ref, low_ref, high_ref, before_ref, top_ref):
+    @pl.when(pl.program_id(0) == 0)
+    def _():
+        top_ref[...] = before_ref[...]
+
+    top = jnp.max(jnp.abs(latest(weight_ref, low_ref, high_ref)), axis=0, keepdims=True)
+    top_ref[...] = jnp.maximum(top_ref[...], top)
+
+
+def ready_kernel(tiles, n, place_ref, *refs):
+    blocks, (low_ref, high_ref, scale_ref, ready_ref) = refs[:n], refs[n:]
+    for b in range(n):
+
+        @pl.when(pl.program_id(0) // tiles == b)
+        def _():
+            ready_ref[...] = (
+                latest(blocks[b], low_ref, high_ref) * (1.0 / scale_ref[...])
+            ).astype(jnp.bfloat16)
+
+
+def column_top(place, block, low_all, high, before, tile):
+    rows, cols = block.shape
+    rank = low_all.shape[1]
+    tiles = rows // tile
+    return pl.pallas_call(
+        top_kernel,
+        grid_spec=pltpu.PrefetchScalarGridSpec(
+            num_scalar_prefetch=1,
+            grid=(tiles,),
+            in_specs=[
+                pl.BlockSpec((tile, cols), lambda i, p: (i, 0)),
+                pl.BlockSpec((tile, rank), lambda i, p: (p[0] * tiles + i, 0)),
+                pl.BlockSpec((rank, cols), lambda i, p: (0, 0)),
+                pl.BlockSpec((1, cols), lambda i, p: (0, 0)),
+            ],
+            out_specs=pl.BlockSpec((1, cols), lambda i, p: (0, 0)),
+        ),
+        out_shape=jax.ShapeDtypeStruct((1, cols), jnp.float32),
+        cost_estimate=pl.CostEstimate(
+            flops=2 * rows * cols * rank, bytes_accessed=2 * rows * cols, transcendentals=0
+        ),
+        name="column_top",
+    )(place.reshape(1), block, low_all, high, before)
+
+
+def place_ready(places, blocks, low_all, high, scale, tile):
+    n = len(blocks)
+    rows, cols = blocks[0].shape
+    rank = low_all.shape[1]
+    tiles = rows // tile
+
+    def own_tile(b):
+        return lambda s, p: (jnp.clip(s - b * tiles, 0, tiles - 1), 0)
+
+    def row_tile(s, p):
+        return (p[s // tiles] * tiles + s % tiles, 0)
+
+    return pl.pallas_call(
+        functools.partial(ready_kernel, tiles, n),
+        grid_spec=pltpu.PrefetchScalarGridSpec(
+            num_scalar_prefetch=1,
+            grid=(n * tiles,),
+            in_specs=[pl.BlockSpec((tile, cols), own_tile(b)) for b in range(n)]
+            + [
+                pl.BlockSpec((tile, rank), row_tile),
+                pl.BlockSpec((rank, cols), lambda s, p: (0, 0)),
+                pl.BlockSpec((1, cols), lambda s, p: (0, 0)),
+            ],
+            out_specs=pl.BlockSpec((tile, cols), row_tile),
+        ),
+        out_shape=jax.ShapeDtypeStruct((n * rows, cols), jnp.bfloat16),
+        cost_estimate=pl.CostEstimate(
+            flops=2 * n * rows * cols * rank,
+            bytes_accessed=4 * n * rows * cols,
+            transcendentals=0,
+        ),
+        name="place_ready",
+    )(jnp.stack(places), *blocks, low_all, high, scale)
+
+
+def by_permutes(n, wide, weight_up, low_up, high_up, norm_train, norm_step):
+    me = lax.axis_index("zero")
+    rows, all_cols = weight_up.shape
+    cols, rank = all_cols // n, low_up.shape[1]
+    share = rows // wide
+    norm = (norm_train + norm_step).astype(jnp.bfloat16)
+    part = lax.dynamic_slice_in_dim(low_up, lax.axis_index("width") * share, share)
+    sent = jnp.concatenate([part.reshape(-1), norm])
+    gathered = lax.all_gather(sent, ("zero", "width"), axis=0, tiled=False)
+    low_all = gathered[:, : share * rank].reshape(n * rows, rank)
+    serve_norm = gathered[:, share * rank :].reshape(-1)
+    high = lax.dynamic_slice_in_dim(high_up, me * cols, cols, axis=1) * jnp.bfloat16(mix_rate)
+
+    blocks, places = [], []
+    for k in range(1, n):
+        target = lax.rem(me + k, n)
+        block = lax.dynamic_slice_in_dim(weight_up, target * cols, cols, axis=1)
+        block, weight_up = lax.optimization_barrier((block, weight_up))
+        blocks.append(lax.ppermute(block, "zero", [(i, (i + k) % n) for i in range(n)]))
+        places.append(lax.rem(me + n - k, n))
+    blocks.insert(0, lax.dynamic_slice_in_dim(weight_up, me * cols, cols, axis=1))
+    places.insert(0, me)
+    tile = rows // 6 if rows % 96 == 0 else rows // 4
+    scale = jnp.zeros((1, cols), jnp.float32)
+    for b, p in zip(blocks, places):
+        scale = column_top(p, b, low_all, high, scale, tile)
+    ready = place_ready(places, blocks, low_all, high, scale, tile)
+    return ready, scale.reshape(-1), serve_norm
+
+
+def by_exchange(weight_up, low_up, high_up, norm_train, norm_step):
     latest_up = weight_up.astype(jnp.float32) + mix_rate * jnp.dot(
         low_up, high_up, preferred_element_type=jnp.float32
     )
@@ -22,6 +143,15 @@
 
 
 def solution(mesh):
+    n, wide = mesh.shape["zero"], mesh.shape["width"]
+
+    def shards(weight_up, low_up, high_up, norm_train, norm_step):
+        rows, all_cols = weight_up.shape
+        given = (weight_up, low_up, high_up, norm_train, norm_step)
+        if n <= 16 and all_cols % (n * 128) == 0 and rows % (64 * wide) == 0:
+            return by_permutes(n, wide, *given)
+        return by_exchange(*given)
+
     return jax.shard_map(
         shards,
         mesh=mesh,

time: 1000 us -> 985 us (0.985)
  blocking collectives: 863 us -> 0 us
  waiting for transfers between devices: 0.01 us -> 813 us
  Pallas kernels: 0 us -> 92.8 us
  matrix products: 37.4 us -> 0 us
  other arithmetic: 36.6 us -> 2.96 us
  between operations: 0.66 us -> 14.2 us
    all_gather x1 -> x0, blocking collectives: 837 us -> none  [shards(): lax.all_gather((norm_train + norm_step).astype(jnp.bfloat16), ('zero', 'w...]
    all_gather x0 -> x1, waiting for transfers between devices: none -> 640 us  [by_permutes(): gathered = lax.all_gather(sent, ('zero', 'width'), axis=0, tiled=False)]
    ppermute x0 -> x7, waiting for transfers between devices: none -> 173 us  [by_permutes(): lax.ppermute(block, 'zero', [(i, (i + k) % n) for i in range(n)])]
    pallas_call x0 -> x9, Pallas kernels: none -> 92.8 us  [the longest x1 47.6 us: place_ready(): pl.pallas_call(functools.partial(ready_kernel, tiles, n), grid_spec=pltpu...]
    dynamic_slice x1 -> x10, local copies, waits for them, and re-layouts: 0.67 us -> 38.7 us  [the longest x7 33.8 us: by_permutes(): block = lax.dynamic_slice_in_dim(weight_up, target * cols, cols, axis=1)]
    dot_general x1 -> x0, matrix products: 37.4 us -> none  [shards(): jnp.dot(low_up, high_up, preferred_element_type=jnp.float32)]
    convert_element_type x2 -> x1, other arithmetic: 36.5 us -> 0.01 us  [by_permutes(): norm = (norm_train + norm_step).astype(jnp.bfloat16)]
    all_to_all x1 -> x0, local copies, waits for them, and re-layouts: 26 us -> none  [shards(): lax.all_to_all(narrow_up, 'zero', split_axis=1, concat_axis=0, tiled=True)]
  transfers between devices with their start and end apart: 1 -> 8, of which waited for: 0 -> 3; matrix products, arithmetic and copies ran while one was open for 0% -> 4% of each run, Pallas kernels for 0% -> 4%
where the time goes in v1:
time: 985 us; the launch traced here: 979 us
  waiting for transfers between devices  813 us (83%)
  Pallas kernels  92.8 us (9%)
  local copies, waits for them, and re-layouts  47.9 us (5%)
  between operations  14.2 us (1%)
    all_gather x1, waiting for transfers between devices, by_permutes(): gathered = lax.all_gather(sent, ('zero', 'width'), axis=0, tiled=False)  640 us
    ppermute x7, waiting for transfers between devices, by_permutes(): lax.ppermute(block, 'zero', [(i, (i + k) % n) for i in range(n)])  173 us
    pallas_call x1, Pallas kernels, place_ready(): pl.pallas_call(functools.partial(ready_kernel, tiles, n), grid_spec=pltpu...  47.6 us
    pallas_call x8, Pallas kernels, column_top(): pl.pallas_call(top_kernel, grid_spec=pltpu.PrefetchScalarGridSpec(num_sca...  45.2 us
    dynamic_slice x7, local copies, waits for them, and re-layouts, by_permutes(): block = lax.dynamic_slice_in_dim(weight_up, target * cols, cols, axis=1)  33.8 us
  transfers between devices with their start and end apart: 8, of which 3 were waited for; matrix products, arithmetic and copies ran while one was open for 4% of the time, Pallas kernels for 4%

profile of v1, /device:TPU:17, one launch (start us, length us, event | category | flops | bytes accessed | tf_op | source)
XLA Modules:
  0.0 979.2 jit_solution(12730368125303124270)
XLA Ops:
  7.2 0.0 copy-start
  7.2 0.0 all-gather.4.cloned.1.call-start
  7.2 4.9 constant_dynamic-slice_fusion.8
  12.1 4.9 constant_dynamic-slice_fusion.7
  17.0 1.2 collective-permute-start.1
  18.3 1.3 collective-permute-start
  19.5 4.7 constant_dynamic-slice_fusion.6
  24.3 4.7 constant_dynamic-slice_fusion.5
  29.0 4.9 constant_dynamic-slice_fusion.4
  33.9 4.8 constant_dynamic-slice_fusion.3
  38.7 0.2 collective-permute-start.5
  38.9 2.7 collective-permute-start.4
  41.6 0.6 collective-permute-start.3
  42.2 0.0 copy-start.2
  42.2 0.0 copy-start.3
  42.2 78.0 %collective-permute-done.1.weight_ref.refs_2_ = bf16[1536,1536]{1,0:T(8,128)(2,1)} collective-permute-done((bf16[1536,1536]{1,0:T(8,128)(2,1)}, bf16[1536,1536]{1,0:T(8,128)(2,1)}, u32[]{:S(2)}, u32[]{:S(2)}) %collective-permute-start.1) | collective-permute-done | bytes 4718624 | tf_op jit(solution)/shard_map/ppermute | solution.py:118
  120.2 2.0 collective-permute-start.2
  122.2 4.8 constant_dynamic-slice_fusion.2
  127.0 95.2 %collective-permute-done.weight_ref.refs_1_ = bf16[1536,1536]{1,0:T(8,128)(2,1)} collective-permute-done((bf16[1536,1536]{1,0:T(8,128)(2,1)}, bf16[1536,1536]{1,0:T(8,128)(2,1)}, u32[]{:S(2)}, u32[]{:S(2)}) %collective-permute-start) | collective-permute-done | bytes 4718624 | tf_op jit(solution)/shard_map/ppermute | solution.py:118
  222.2 0.0 collective-permute-start.6
  222.2 0.0 copy-done
  222.2 0.1 copy.10
  222.3 0.1 reshape.10
  222.5 0.0 copy-done.2
  222.5 0.0 copy-done.3
  222.5 0.7 reshape.31
  223.2 0.0 all-gather.4.cloned.1.call-update
  223.2 0.6 stack.35.place_ref
  223.9 1.6 dynamic-slice_multiply_fusion.high_ref.refs_9_
  225.5 4.9 constant_dynamic-slice_fusion.1.weight_ref.refs_0_
  230.3 640.1 %all-gather.4.cloned.1.call-done = bf16[32,1,24960]{2,1,0:T(2,128)(2,1)} async-done(((bf16[1,1,24960]{2,1,0:T(2,128)(2,1)}), bf16[32,1,24960]{2,1,0:T(2,128)(2,1)}) %all-gather.4.cloned.1.call-update) | async-done | bytes 1597456 | tf_op jit(solution)/shard_map/all_gather | solution.py:108
  870.5 2.1 copy.13
  872.5 0.1 slice.8
  872.7 0.6 reshape.26
  873.3 4.3 reshape.24.low_ref.refs_8_
  877.6 0.6 broadcast_in_dim.3.before_ref
  878.2 5.6 column_top.8.before_ref
  883.9 5.6 column_top.9.before_ref
  889.5 5.6 column_top.10.before_ref
  895.1 0.0 collective-permute-done.2.weight_ref.refs_3_
  895.2 5.7 column_top.11.before_ref
  900.8 0.0 collective-permute-done.3.weight_ref.refs_4_
  900.8 5.7 column_top.12.before_ref
  906.5 0.0 collective-permute-done.4.weight_ref.refs_5_
  906.5 5.7 column_top.13.before_ref
  912.1 0.0 collective-permute-done.5.weight_ref.refs_6_
  912.1 5.7 column_top.14.before_ref
  917.8 0.0 collective-permute-done.6.weight_ref.refs_7_
  917.8 5.7 column_top.15.refs_10_
  923.4 1.3 reduce
  924.8 0.0 copy-start.1
  924.8 47.6 %place_ready.1 = bf16[12288,1536]{1,0:T(8,128)(2,1)} custom-call(s32[8]{0:T(128)} %stack.35.place_ref, bf16[1536,1536]{1,0:T(8,128)(2,1)} %constant_dynamic-slice_fusion.1.weight_ref.refs_0_, bf16[1536,1536]{1,0:T(8,128)(2,1)} %collective-permute-done.weight_ref.refs_1_, bf16[1536,1536]{1,0:T(8,128)(2,1)} %collective-permute-done.1.weight_ref.refs_2_, ...), custom_call_target="tpu_custom_call" | custom-call | flops 2415919104 | bytes 75497472 | tf_op jit(solution)/shard_map/place_ready/pallas_call | solution.py:77
  972.4 0.0 copy-done.1
  (4 shorter events, 0.0 us)
Async XLA Ops:
  7.2 215.0 %copy-start = (bf16[1536,64]{0,1:T(8,128)(2,1)S(1)}, bf16[1536,64]{0,1:T(8,128)(2,1)}, u32[]{:S(2)}) copy-start(bf16[1536,64]{0,1:T(8,128)(2,1)} %param.6) | copy-start | bytes 589828
  7.2 863.3 %all-gather.4.cloned.1.call-start = ((), (), s32[]{:S(2)}) async-start(), calls=%async_computation | async-start | bytes 3294720 | tf_op jit(solution)/shard_map/all_gather | solution.py:108
  17.0 103.2 %collective-permute-start.1 = (bf16[1536,1536]{1,0:T(8,128)(2,1)}, bf16[1536,1536]{1,0:T(8,128)(2,1)}, u32[]{:S(2)}, u32[]{:S(2)}) collective-permute-start(bf16[1536,1536]{1,0:T(8,128)(2,1)} %constant_dynamic-slice_fusion.7), channel_id=1, source_target_pairs={{0,8},{4,12},{8,16},{12,20},{16,24},{20,28},{24,0},{28,4},{1,9},{5... | collective-permute-start | bytes 14155784 | tf_op jit(solution)/shard_map/ppermute | solution.py:118
  18.3 203.9 %collective-permute-start = (bf16[1536,1536]{1,0:T(8,128)(2,1)}, bf16[1536,1536]{1,0:T(8,128)(2,1)}, u32[]{:S(2)}, u32[]{:S(2)}) collective-permute-start(bf16[1536,1536]{1,0:T(8,128)(2,1)} %constant_dynamic-slice_fusion.8), channel_id=1, source_target_pairs={{0,4},{4,8},{8,12},{12,16},{16,20},{20,24},{24,28},{28,0},{1,5},{5... | collective-permute-start | bytes 14155784 | tf_op jit(solution)/shard_map/ppermute | solution.py:118
  38.7 873.4 %collective-permute-start.5 = (bf16[1536,1536]{1,0:T(8,128)(2,1)}, bf16[1536,1536]{1,0:T(8,128)(2,1)}, u32[]{:S(2)}, u32[]{:S(2)}) collective-permute-start(bf16[1536,1536]{1,0:T(8,128)(2,1)} %constant_dynamic-slice_fusion.3), channel_id=1, source_target_pairs={{0,24},{4,28},{8,0},{12,4},{16,8},{20,12},{24,16},{28,20},{1,25},{... | collective-permute-start | bytes 14155784 | tf_op jit(solution)/shard_map/ppermute | solution.py:118
  38.9 867.6 %collective-permute-start.4 = (bf16[1536,1536]{1,0:T(8,128)(2,1)}, bf16[1536,1536]{1,0:T(8,128)(2,1)}, u32[]{:S(2)}, u32[]{:S(2)}) collective-permute-start(bf16[1536,1536]{1,0:T(8,128)(2,1)} %constant_dynamic-slice_fusion.4), channel_id=1, source_target_pairs={{0,20},{4,24},{8,28},{12,0},{16,4},{20,8},{24,12},{28,16},{1,21},{... | collective-permute-start | bytes 14155784 | tf_op jit(solution)/shard_map/ppermute | solution.py:118
  41.6 859.2 %collective-permute-start.3 = (bf16[1536,1536]{1,0:T(8,128)(2,1)}, bf16[1536,1536]{1,0:T(8,128)(2,1)}, u32[]{:S(2)}, u32[]{:S(2)}) collective-permute-start(bf16[1536,1536]{1,0:T(8,128)(2,1)} %constant_dynamic-slice_fusion.5), channel_id=1, source_target_pairs={{0,16},{4,20},{8,24},{12,28},{16,0},{20,4},{24,8},{28,12},{1,17},{... | collective-permute-start | bytes 14155784 | tf_op jit(solution)/shard_map/ppermute | solution.py:118
  42.2 180.2 %copy-start.2 = (f32[384]{0:T(512)S(1)}, f32[384]{0:T(512)}, u32[]{:S(2)}) copy-start(f32[384]{0:T(512)} %param.8) | copy-start | bytes 4612
  42.2 180.2 %copy-start.3 = (f32[384]{0:T(512)S(1)}, f32[384]{0:T(512)}, u32[]{:S(2)}) copy-start(f32[384]{0:T(512)} %param.9) | copy-start | bytes 4612
  120.2 774.9 %collective-permute-start.2 = (bf16[1536,1536]{1,0:T(8,128)(2,1)}, bf16[1536,1536]{1,0:T(8,128)(2,1)}, u32[]{:S(2)}, u32[]{:S(2)}) collective-permute-start(bf16[1536,1536]{1,0:T(8,128)(2,1)} %constant_dynamic-slice_fusion.6), channel_id=1, source_target_pairs={{0,12},{4,16},{8,20},{12,24},{16,28},{20,0},{24,4},{28,8},{1,13},{... | collective-permute-start | bytes 14155784 | tf_op jit(solution)/shard_map/ppermute | solution.py:118
  222.2 695.6 %collective-permute-start.6 = (bf16[1536,1536]{1,0:T(8,128)(2,1)}, bf16[1536,1536]{1,0:T(8,128)(2,1)}, u32[]{:S(2)}, u32[]{:S(2)}) collective-permute-start(bf16[1536,1536]{1,0:T(8,128)(2,1)} %constant_dynamic-slice_fusion.2), channel_id=1, source_target_pairs={{0,28},{4,0},{8,4},{12,8},{16,12},{20,16},{24,20},{28,24},{1,29},{... | collective-permute-start | bytes 14155784 | tf_op jit(solution)/shard_map/ppermute | solution.py:118
  924.8 47.6 %copy-start.1 = (bf16[1536,64]{0,1:T(8,128)(2,1)S(1)}, bf16[1536,64]{0,1:T(8,128)(2,1)}, u32[]{:S(2)}) copy-start(bf16[1536,64]{0,1:T(8,128)(2,1)} %param.6) | copy-start | bytes 589828
Sparse Core Ops, SparseCore 0:
  223.3 647.0 all-gather.3
